TPU v7x, 128 devices: a whole 4x4x4 slice. The times are simulated.
128 devices in a mesh: pair: 2 (over core), shard: 64 (over z, y, x).
Axes of the slice: x: 4, y: 4, z: 4, core: 2. Of those that a mesh axis runs over, the one named last changes fastest.
Arguments:
- master: float32 [3072, 4096], P('shard', 'pair'), may hold values from -1.5 to 1.5
- gradient: float32 [3072, 4096], P('shard', 'pair'), may hold values from -40 to 40
- first_moment: float32 [3072, 4096], P('shard', 'pair'), may hold values from -4 to 4
- second_moment: float32 [3072, 4096], P('shard', 'pair'), may hold values from 0.02 to 4
- max_norm: float32 [1], replicated, may hold values from 768 to 1536
- step_count: int32 [1], replicated, may hold values from 1 to 1000
Outputs:
- new_master: float32 [3072, 4096], P('shard', 'pair')
- new_first: float32 [3072, 4096], P('shard', 'pair')
- new_second: float32 [3072, 4096], P('shard', 'pair')
- compute_codes: bfloat16 [3072, 4096], P('pair')
- block_scales: bfloat16 [3072, 128], P('pair')
All inputs are finite; a program needn't handle non-finite values.
Results may differ from a plain program's by a relative error of at most 0.001.
The roundings to bfloat16 on the way count: a program that leaves them out, or rounds other values in their place, can miss the bound.
Values may be sent and summed in bfloat16 or wider, within the bound.
A program may use at most 192 MiB of HBM per device.

v0:
```python
import functools

import jax
import jax.numpy as jnp
from jax import lax
from jax.sharding import Mesh
from jax.sharding import PartitionSpec as P

BLOCK = 32
PAIR_SHARD = ("pair", "shard_0", "shard_1", "shard_2")
SHARD = ("shard_0", "shard_1", "shard_2")


beta_first = 0.9
beta_second = 0.99
learn_rate = 0.01
decay_rate = 0.1
adam_eps = 1e-06
scale_floor = 0.25


def by_axis(x, axes):
    return functools.reduce(lax.psum, axes, x)


def side_by_side(arrays, axis, dim, along):
    widths = [a.shape[along] for a in arrays]
    both = jnp.concatenate(arrays, axis=along)
    whole = lax.all_gather(both, axis, axis=dim, tiled=True)
    return tuple(jnp.split(whole, [sum(widths[:k]) for k in range(1, len(widths))], axis=along))


def quantize(weights):
    height, width = weights.shape
    blocked = weights.reshape(height, width // BLOCK, BLOCK)
    largest = jnp.max(jnp.abs(blocked), axis=2)
    scales = jnp.maximum(largest, scale_floor).astype(jnp.bfloat16)
    divided = blocked / scales.astype(jnp.float32)[:, :, None]
    return (divided.astype(jnp.bfloat16).reshape(height, width), scales)


def adam_update(master, gradient, first_moment, second_moment, max_norm, step_count, squares):
    norm_limit = max_norm[0]
    clip_factor = norm_limit / jnp.maximum(jnp.sqrt(squares), norm_limit)
    clipped = clip_factor * gradient
    new_first = beta_first * first_moment + (1.0 - beta_first) * clipped
    new_second = beta_second * second_moment + (1.0 - beta_second) * clipped * clipped
    counted = step_count[0].astype(jnp.float32)
    first_fix = 1.0 - jnp.power(jnp.full((), beta_first, jnp.float32), counted)
    second_fix = 1.0 - jnp.power(jnp.full((), beta_second, jnp.float32), counted)
    update = (
        new_first / first_fix / (jnp.sqrt(new_second / second_fix) + adam_eps) + decay_rate * master
    )
    new_master = master - learn_rate * update
    return (new_master, new_first, new_second)


def per_device(master, gradient, first_moment, second_moment, max_norm, step_count):
    squares = by_axis(jnp.sum(gradient * gradient), PAIR_SHARD)
    new_master, new_first, new_second = adam_update(
        master, gradient, first_moment, second_moment, max_norm, step_count, squares
    )
    own_codes, own_scales = quantize(new_master)
    half_codes, half_scales = side_by_side((own_codes, own_scales), SHARD, 0, 1)
    compute_codes, block_scales = (
        lax.all_to_all(half_codes, "pair", split_axis=0, concat_axis=1, tiled=True),
        lax.all_to_all(half_scales, "pair", split_axis=0, concat_axis=1, tiled=True),
    )
    return (new_master, new_first, new_second, compute_codes, block_scales)


def solution(mesh):
    finer = Mesh(
        mesh.devices.reshape(mesh.shape["pair"], 4, 4, 4), ("pair", "shard_0", "shard_1", "shard_2")
    )
    return jax.shard_map(
        per_device,
        mesh=finer,
        in_specs=(P(SHARD, "pair"), P(SHARD, "pair"), P(SHARD, "pair"), P(SHARD, "pair"), P(), P()),
        out_specs=(
            P(SHARD, "pair"),
            P(SHARD, "pair"),
            P(SHARD, "pair"),
            P("pair", None),
            P("pair", None),
        ),
        check_vma=False,
    )
```

profile of v0, /device:TPU:1, one launch (start us, length us, event | category | flops | bytes accessed | tf_op | source)
XLA Modules:
  0.0 180.7 jit_solution(10046411327130101497)
XLA Ops:
  7.2 0.0 all-gather.2.cloned.1.call-start
  7.9 1.7 multiply_reduce_fusion
  9.6 4.1 %psum.28 = f32[]{:T(128)} all-reduce(f32[]{:T(128)} %multiply_reduce_fusion), channel_id=1, replica_groups=mesh['pair'=2,'shard_0'=4,'shard_1'=4,'shard_2'=4] {'pair'}, use_global_device_ids=true, to_apply=%region_1.0 | all-reduce | flops 1 | bytes 8 | tf_op jit(solution)/shard_map/psum | solution.py:23
  13.8 10.5 %psum.29 = f32[]{:T(128)} all-reduce(f32[]{:T(128)} %psum.28), channel_id=1, replica_groups=mesh['pair'=2,'shard_0'=4,'shard_1'=4,'shard_2'=4] {'shard_0'}, use_global_device_ids=true, to_apply=%region_2.0 | all-reduce | flops 1 | bytes 8 | tf_op jit(solution)/shard_map/psum | solution.py:23
  24.3 9.3 %psum.30 = f32[]{:T(128)} all-reduce(f32[]{:T(128)} %psum.29), channel_id=1, replica_groups=mesh['pair'=2,'shard_0'=4,'shard_1'=4,'shard_2'=4] {'shard_1'}, use_global_device_ids=true, to_apply=%region_3.0 | all-reduce | flops 1 | bytes 8 | tf_op jit(solution)/shard_map/psum | solution.py:23
  34.3 9.1 %psum.31 = f32[]{:T(128)} all-reduce(f32[]{:T(128)} %psum.30), channel_id=1, replica_groups=mesh['pair'=2,'shard_0'=4,'shard_1'=4,'shard_2'=4] {'shard_2'}, use_global_device_ids=true, to_apply=%region_4.0 | all-reduce | flops 1 | bytes 8 | tf_op jit(solution)/shard_map/psum | solution.py:23
  44.1 2.5 %fusion.1 = (bf16[48,2048]{1,0:T(8,128)(2,1)S(1)}, f32[48,2048]{1,0:T(8,128)S(1)}, f32[48,2048]{1,0:T(8,128)}, f32[48,2048]{1,0:T(8,128)}) fusion(f32[48,2048]{1,0:T(8,128)} %param.6, f32[]{:T(128)} %bitcast.2, f32[]{:T(128)} %bitcast.1, f32[48,2048]{1,0:T(8,128)} %param.7, f32[]{:T(128)S(6)} %div.27, f32[48,2048]{1,0:T(8,128)} %param.9, f32[48,2048]{1,0:T(8,128)} %param.8), kind=kLoop, calls=%fused_computation.8 | loop fusion | flops 1769472 | bytes 2949132 | tf_op jit(solution)/shard_map/abs | solution.py:36
  46.6 0.0 copy-start
  46.7 0.6 abs.7
  47.2 0.5 reduce_max.9
  47.7 0.5 div.32
  48.2 0.7 div.33
  48.9 0.1 divide_convert_fusion
  49.0 0.7 pad_maximum_fusion
  49.7 0.0 all-gather.2.cloned.1.call-update
  49.7 93.8 %all-gather.2.cloned.1.call-done = bf16[3072,2112]{1,0:T(8,128)(2,1)} async-done(((bf16[48,2112]{1,0:T(8,128)(2,1)}), bf16[3072,2112]{1,0:T(8,128)(2,1)}) %all-gather.2.cloned.1.call-update) | async-done | bytes 12976144 | tf_op jit(solution)/shard_map/all_gather | solution.py:29
  143.5 1.2 split.9
  144.7 0.3 copy.14
  144.9 4.5 %all_to_all.38 = bf16[2,1536,64]{1,2,0:T(8,128)(2,1)S(1)} all-to-all(bf16[2,1536,64]{1,2,0:T(8,128)(2,1)S(1)} %copy.14), channel_id=1, replica_groups=mesh['pair'=2,'shard_0'=4,'shard_1'=4,'shard_2'=4] {'pair'}, dimensions={0} | all-to-all | bytes 786432 | tf_op jit(solution)/shard_map/all_to_all | solution.py:67
  149.4 0.9 copy.15
  150.4 0.0 slice-start
  150.4 0.0 copy-done
  150.4 4.6 %slice-done = bf16[3072,2048]{1,0:T(8,128)(2,1)S(1)} async-done(((bf16[3072,2112]{1,0:T(8,128)(2,1)}), bf16[3072,2048]{1,0:T(8,128)(2,1)S(1)}, s32[]{:S(2)}) %slice-start) | async-done | bytes 12582936 | tf_op jit(solution)/shard_map/split | solution.py:30
  154.9 13.8 %all_to_all.39 = bf16[2,1536,2048]{2,1,0:T(8,128)(2,1)S(1)} all-to-all(bf16[2,1536,2048]{2,1,0:T(8,128)(2,1)S(1)} %bitcast.13), channel_id=1, replica_groups=mesh['pair'=2,'shard_0'=4,'shard_1'=4,'shard_2'=4] {'pair'}, dimensions={0} | all-to-all | bytes 25165824 | tf_op jit(solution)/shard_map/all_to_all | solution.py:66
  168.8 5.0 %copy.16 = bf16[2,192,8,2048]{3,2,0,1:T(8,128)(2,1)} copy(bf16[2,192,8,2048]{3,2,1,0:T(8,128)(2,1)S(1)} %bitcast.14) | data formatting | bytes 25165824 | tf_op jit(solution)/shard_map/all_to_all | solution.py:66
  (1 shorter events, 0.0 us)
Async XLA Ops:
  7.2 136.3 %all-gather.2.cloned.1.call-start = ((), (), s32[]{:S(2)}) async-start(), calls=%async_computation.2 | async-start | bytes 13578240 | tf_op jit(solution)/shard_map/all_gather | solution.py:29
  46.6 103.7 %copy-start = (f32[48,2048]{1,0:T(8,128)}, f32[48,2048]{1,0:T(8,128)S(1)}, u32[]{:S(2)}) copy-start(f32[48,2048]{1,0:T(8,128)S(1)} %get-tuple-element.11) | copy-start | bytes 1179652
  150.4 4.6 %slice-start = ((bf16[3072,2112]{1,0:T(8,128)(2,1)}), bf16[3072,2048]{1,0:T(8,128)(2,1)S(1)}, s32[]{:S(2)}) async-start(bf16[3072,2112]{1,0:T(8,128)(2,1)} %all-gather.2.cloned.1.call-done), calls=%async_computation.3 | async-start | bytes 25165824 | tf_op jit(solution)/shard_map/split | solution.py:30
Sparse Core Ops, SparseCore 0:
  49.8 93.5 all-gather.1
where the time goes:
time: 181 us
  waiting for transfers between devices  93.8 us (52%)
  blocking collectives  51.4 us (28%)
  between operations  16.2 us (9%)
  local copies, waits for them, and re-layouts  13.7 us (8%)
  other arithmetic  5.51 us (3%)
    all_gather x1, waiting for transfers between devices, side_by_side(): whole = lax.all_gather(both, axis, axis=dim, tiled=True)  93.8 us
    psum x4, blocking collectives, by_axis(): return functools.reduce(lax.psum, axes, x)  33.1 us
    all_to_all x1, blocking collectives, per_device(): lax.all_to_all(half_codes, 'pair', split_axis=0, concat_axis=1, tiled=True)  13.8 us
    split x3, local copies, waits for them, and re-layouts, side_by_side(): jnp.split(whole, [sum(widths[:k]) for k in range(1, len(widths))], axis=a...  5.76 us
    all_to_all x1, local copies, waits for them, and re-layouts, per_device(): lax.all_to_all(half_codes, 'pair', split_axis=0, concat_axis=1, tiled=True)  5.05 us
    all_to_all x1, blocking collectives, per_device(): lax.all_to_all(half_scales, 'pair', split_axis=0, concat_axis=1, tiled=True)  4.52 us
  transfers between devices with their start and end apart: 1, of which 1 were waited for; matrix products, arithmetic and copies ran while one was open for 0% of the time, Pallas kernels for 0%

commit v1 on v0

v1 whole, which is shorter than its diff:
```python
import functools
import heapq
import itertools

import jax
import jax.numpy as jnp
import numpy as np
from jax import lax
from jax.experimental import pallas as pl
from jax.experimental.pallas import tpu as pltpu
from jax.sharding import PartitionSpec as P

MESH = pl.DeviceIdType.MESH
F32, BF16 = jnp.float32, jnp.bfloat16

beta_first = 0.9
beta_second = 0.99
learn_rate = 0.01
decay_rate = 0.1
adam_eps = 1e-06
scale_floor = 0.25

BLOCK = 32
PART = 16
LANES = 128
ORDERS = ((0, 1, 2), (1, 2, 0), (2, 0, 1))


def hops(part, plane, off):
    order = ORDERS[part]
    last = max([j for j, d in enumerate(order) if off[d]], default=-1)
    out = []
    if last >= 0:
        d = order[last]
        swap = d == 2 and plane == 1
        if off[d] == 1:
            out.append((d, 1, 2 if swap else 1))
        if off[d] == 3:
            out.append((d, -1, 1 if swap else 2))
    for d in order[last + 1 :]:
        out += [(d, 1, 0), (d, -1, 0)]
    return out


def arrivals(unit=1.45, latency=1.7, ready=(0.6, 1.2, 1.8)):
    queues = {(r, d, s): [] for r in range(4) for d in range(3) for s in (1, -1)}
    heads, events, count, now = {}, [], itertools.count(), 0.0
    got = {r: {} for r in range(4)}
    order = {r: [] for r in range(4)}
    for r in (0, 1):
        for p in range(3):
            heapq.heappush(events, (ready[p], next(count), r, (p, r, 0, 0), 0))
    while True:
        for k in queues:
            if k not in heads and queues[k]:
                item = queues[k].pop(0)
                heads[k] = [unit if item[1] == 0 else unit / 2, item]
        rate = {k: 0.5 if ((k[0] + 2) % 4, k[1], k[2]) in heads else 1.0 for k in heads}
        times = [now + heads[k][0] / rate[k] for k in heads] + ([events[0][0]] if events else [])
        if not times:
            return order
        then = min(times)
        for k in heads:
            heads[k][0] -= (then - now) * rate[k]
        now = then
        for k in list(heads):
            if heads[k][0] <= 1e-9:
                (r, d, s), ((p, plane, ox, oy), half) = k, heads.pop(k)[1]
                if d == 0:
                    ox = (ox + s) % 4
                elif d == 1:
                    oy = (oy + s) % 4
                else:
                    r = (r + s) % 4
                heapq.heappush(events, (now + latency, next(count), r, (p, plane, ox, oy), half))
        while events and events[0][0] <= now + 1e-9:
            _, _, r, chunk, half = heapq.heappop(events)
            p, plane, ox, oy = chunk
            off = (ox, oy, (r - plane) % 4)
            if off != (0, 0, 0):
                order[r].append((chunk, half))
            seen = got[r].setdefault(chunk, set())
            seen.add(half)
            if 0 in seen or len(seen) == 2:
                for d, s, h in hops(p, plane, off):
                    queues[(r, d, s)].append((chunk, h))


def slot(chunk, half):
    p, plane, ox, oy = chunk
    return (((p * 2 + plane) * 4 + ox) * 4 + oy) * 2 + (half == 2)


SLOTS = 3 * 2 * 4 * 4 * 2


def gather_kernel(
    max_norm,
    step_count,
    master,
    gradient,
    first,
    second,
    new_master,
    new_first,
    new_second,
    whole,
    own,
    other,
    sums,
    sum_rx,
    load_sem,
    swap_sem,
    sum_send,
    sum_recv,
    send_sem,
    recv_sem,
):
    rows, width = own.shape[1:]
    parts = rows // PART
    cols = 2 * width
    full = whole.shape[1]
    cut = LANES * ((full // LANES + 1) // 2)

    me = lax.axis_index("shard")
    core = lax.axis_index("pair")
    x, y, z = lax.rem(me, 4), lax.rem(lax.div(me, 4), 4), lax.div(me, 16)
    role = lax.rem(z + 2 * core, 4)
    source = role < 2
    flip = jnp.logical_or(role == 1, role == 2)
    sigma = jnp.where(flip, -1, 1)

    def at(xx, yy, zz):
        return lax.rem(zz, 4) * 16 + lax.rem(yy, 4) * 4 + lax.rem(xx, 4)

    partner = (1 - core, me)
    x_peers = [(k, at(x + dx, y, z)) for dx in (1, 2, 3) for k in (core, 1 - core)] + [partner]
    y_peers = [(core, at(x, y + d, z)) for d in (1, 2, 3)]
    z_peers = [(core, at(x, y, z + d)) for d in (1, 2, 3)]
    barrier = pltpu.get_barrier_semaphore()
    peers = x_peers + y_peers + z_peers
    for peer in peers:
        pl.semaphore_signal(barrier, inc=1, device_id=peer, device_id_type=MESH)

    loads = [
        pltpu.make_async_copy(ref, own.at[k], load_sem.at[k])
        for k, ref in enumerate((gradient, first, second, master))
    ]
    for load in loads:
        load.start()
    loads[0].wait()
    acc = jnp.zeros((8, LANES), F32)
    for i in range(0, rows, 8):
        for j in range(0, width, LANES):
            g = own[0, i : i + 8, j : j + LANES]
            acc = acc + g * g
    sums[0] = acc
    for load in loads[1:]:
        load.wait()
    pl.semaphore_wait(barrier, len(peers))

    def exchange(step, base, to):
        copies = [
            pltpu.make_async_remote_copy(
                src_ref=sums.at[step],
                dst_ref=sum_rx.at[base + k],
                send_sem=sum_send.at[base + k],
                recv_sem=sum_recv.at[base + k],
                device_id=peer,
                device_id_type=MESH,
            )
            for k, peer in enumerate(to)
        ]
        for copy in copies:
            copy.start()
        return copies

    swaps = [
        pltpu.make_async_remote_copy(
            src_ref=own.at[k],
            dst_ref=other.at[k],
            send_sem=swap_sem.at[k],
            recv_sem=swap_sem.at[4 + k],
            device_id=partner,
            device_id_type=MESH,
        )
        for k in range(4)
    ]

    copies = []
    base = 0
    for step, to in enumerate((x_peers, y_peers, z_peers)):
        started = exchange(step, base, to)
        if step == 0:

            @pl.when(jnp.logical_not(source))
            def _():
                for swap in swaps:
                    swap.start()

        for k, copy in enumerate(started):
            copy.wait_recv()
        acc = sums[step]
        for k in range(len(to)):
            acc = acc + sum_rx[base + k]
        base += len(to)
        copies += started
        if step < 2:
            sums[step + 1] = acc

    squares = jnp.sum(acc, axis=(0, 1), keepdims=True)
    limit = jnp.full((1, 1), max_norm[0], F32)
    clip = limit / jnp.maximum(jnp.sqrt(squares), limit)
    counted = jnp.full((1, 1), step_count[0], jnp.int32).astype(F32)
    inv_first = 1.0 / (1.0 - jnp.exp(counted * float(np.log(beta_first))))
    inv_second = 1.0 / (1.0 - jnp.exp(counted * float(np.log(beta_second))))
    clip = jnp.broadcast_to(clip, (PART, LANES))
    inv_first = jnp.broadcast_to(inv_first, (PART, LANES))
    inv_second = jnp.broadcast_to(inv_second, (PART, LANES))

    lane = lax.broadcasted_iota(jnp.int32, (PART, LANES), 1)
    bits = [(s, lax.bitwise_and(lane, s) != 0) for s in (1, 2, 4, 8, 16)]
    in_block = lax.bitwise_and(lane, BLOCK - 1)
    to_lane = lax.broadcasted_iota(jnp.int32, (LANES, LANES), 1)
    from_lane = lax.broadcasted_iota(jnp.int32, (LANES, LANES), 0)
    spread = jnp.where(
        lax.div(from_lane, BLOCK) + (LANES // BLOCK) * lax.rem(from_lane, BLOCK) == to_lane, 1.0, 0.0
    ).astype(BF16)

    def adam(held, i, j):
        g, m, v, w = (held[k, pl.ds(i, PART), pl.ds(j, LANES)] for k in range(4))
        clipped = clip * g
        m = beta_first * m + (1.0 - beta_first) * clipped
        v = beta_second * v + (1.0 - beta_second) * clipped * clipped
        update = m * inv_first / (jnp.sqrt(v * inv_second) + adam_eps) + decay_rate * w
        return w - learn_rate * update, m, v

    tiles = width // LANES
    step_tiles = 4

    def store(i, j, w, m, v):
        new_master[pl.ds(i, PART), pl.ds(j, LANES)] = w
        new_first[pl.ds(i, PART), pl.ds(j, LANES)] = m
        new_second[pl.ds(i, PART), pl.ds(j, LANES)] = v

    def quantize(row, half, tile, w, scales):
        largest = jnp.abs(w)
        for s, bit in bits:
            lower = pltpu.roll(largest, s, 1)
            upper = pltpu.roll(largest, LANES - s, 1)
            largest = jnp.maximum(largest, jnp.where(bit, lower, upper))
        scale = jnp.maximum(largest, scale_floor).astype(BF16).astype(F32)
        column = pl.multiple_of(half * width + tile * LANES, LANES)
        whole[pl.ds(row, PART), pl.ds(column, LANES)] = (w / scale).astype(BF16)
        return jnp.where(in_block == half * tiles + tile, scale, scales)

    line = [[(lax.rem(y + 4 - oy, 4) * 4 + lax.rem(x + 4 - ox, 4)) * rows for oy in range(4)] for ox in range(4)]
    plane_row = [jnp.where(flip, 16 * rows, 0), jnp.where(flip, 0, 16 * rows)]
    near = {
        (0, 1): at(x + 1, y, z),
        (0, -1): at(x + 3, y, z),
        (1, 1): at(x, y + 1, z),
        (1, -1): at(x, y + 3, z),
        (2, 1): at(x, y, z + 4 + sigma),
        (2, -1): at(x, y, z + 4 - sigma),
    }
    pieces = {0: pl.ds(0, full), 1: pl.ds(0, cut), 2: pl.ds(cut, full - cut)}

    def place(chunk, half):
        p, plane, ox, oy = chunk
        return whole.at[pl.ds(pl.multiple_of(line[ox][oy] + plane_row[plane] + p * PART, PART), PART), pieces[half]]

    def piece(chunk, half, role_now, d, s, number):
        p, plane, ox, oy = chunk
        if d == 0:
            ox = (ox + s) % 4
        elif d == 1:
            oy = (oy + s) % 4
        elif (role_now == 0) == (s == 1):
            plane = 1 - plane
        ref = place(chunk, half)
        return pltpu.make_async_remote_copy(
            src_ref=ref,
            dst_ref=ref,
            send_sem=send_sem.at[number],
            recv_sem=recv_sem.at[slot((p, plane, ox, oy), half)],
            device_id=(core, near[(d, s)]),
            device_id_type=MESH,
        )

    def landed(chunk, half):
        ref = place(chunk, half)
        pltpu.make_async_remote_copy(
            src_ref=ref,
            dst_ref=ref,
            send_sem=send_sem.at[0],
            recv_sem=recv_sem.at[slot(chunk, half)],
            device_id=(core, near[(0, 1)]),
            device_id_type=MESH,
        ).wait_recv()

    def follow(role_now, order, sent):
        got = {}
        for chunk, half in order:
            landed(chunk, half)
            seen = got.setdefault(chunk, set())
            seen.add(half)
            if 0 in seen or len(seen) == 2:
                p, plane, ox, oy = chunk
                for d, s, h in hops(p, plane, (ox, oy, (role_now - plane) % 4)):
                    copy = piece(chunk, h, role_now, d, s, len(sent))
                    copy.start()
                    sent.append(copy)
        for copy in sent:
            copy.wait_send()

    schedule = arrivals()

    @pl.when(source)
    def _():
        for swap in swaps:
            swap.wait_recv()
        sent = []
        for p in range(parts):
            i = p * PART
            row = pl.multiple_of(line[0][0] + plane_row[0] + i, PART)

            def body(t, scales, i=i, row=row):
                for k in range(step_tiles):
                    tile = t * step_tiles + k
                    j = pl.multiple_of(tile * LANES, LANES)
                    w, m, v = adam(own, i, j)
                    store(i, j, w, m, v)
                    scales = quantize(row, core, tile, w, scales)
                    w, m, v = adam(other, i, j)
                    scales = quantize(row, 1 - core, tile, w, scales)
                return scales

            scales = lax.fori_loop(0, tiles // step_tiles, body, jnp.zeros((PART, LANES), F32))
            moved = jnp.dot(scales.astype(BF16), spread, preferred_element_type=F32)
            whole[pl.ds(row, PART), cols:] = moved.astype(BF16)
            for d, s, h in hops(p, 0, (0, 0, 0)):
                copy = piece((p, 0, 0, 0), h, 0, d, s, len(sent))
                copy.start()
                sent.append(copy)
        follow(0, schedule[0], sent)

    @pl.when(jnp.logical_not(source))
    def _():
        for p in range(parts):
            i = p * PART

            def body(t, carry, i=i):
                for k in range(step_tiles):
                    j = pl.multiple_of((t * step_tiles + k) * LANES, LANES)
                    store(i, j, *adam(own, i, j))
                return carry

            lax.fori_loop(0, tiles // step_tiles, body, 0)
        follow(3, schedule[3], [])
        for swap in swaps:
            swap.wait_send()

    for copy in copies:
        copy.wait_send()


def write_kernel(whole, new_master, new_first, new_second, codes_out, scales_out, master_out, first_out, second_out, sem):
    rows, cols = codes_out.shape
    count = 8
    step = rows // count
    copies = []

    def go(src, dst):
        copy = pltpu.make_async_copy(src, dst, sem.at[len(copies)])
        copy.start()
        copies.append(copy)

    for k in range(count):
        go(whole.at[pl.ds(k * step, step), pl.ds(0, cols)], codes_out.at[pl.ds(k * step, step), :])
    go(whole.at[:, pl.ds(cols, scales_out.shape[1])], scales_out)
    go(new_master, master_out)
    go(new_first, first_out)
    go(new_second, second_out)
    for copy in copies:
        copy.wait()


def per_device(master, gradient, first_moment, second_moment, max_norm, step_count):
    rows, width = master.shape
    cols = 2 * width
    scales = cols // BLOCK
    kept = 32 * rows
    full = cols + scales
    smem = pl.BlockSpec(memory_space=pltpu.SMEM)
    any_spec = pl.BlockSpec(memory_space=pl.ANY)
    vmem = pl.BlockSpec(memory_space=pltpu.VMEM)
    sends = 160
    held = pl.pallas_call(
        gather_kernel,
        out_shape=tuple(pltpu.VMEM((rows, width), F32) for _ in range(3)) + (pltpu.VMEM((kept, full), BF16),),
        in_specs=[smem, smem] + [any_spec] * 4,
        out_specs=tuple(vmem for _ in range(4)),
        scratch_shapes=[
            pltpu.VMEM((4, rows, width), F32),
            pltpu.VMEM((4, rows, width), F32),
            pltpu.VMEM((3, 8, LANES), F32),
            pltpu.VMEM((13, 8, LANES), F32),
            pltpu.SemaphoreType.DMA((4,)),
            pltpu.SemaphoreType.DMA((8,)),
            pltpu.SemaphoreType.DMA((13,)),
            pltpu.SemaphoreType.DMA((13,)),
            pltpu.SemaphoreType.DMA((sends,)),
            pltpu.SemaphoreType.DMA((SLOTS,)),
        ],
        compiler_params=pltpu.CompilerParams(collective_id=0, has_side_effects=True, vmem_limit_bytes=16 * 2**20),
        name="update_and_gather",
    )(
        max_norm,
        step_count,
        *(
            pltpu.with_memory_space_constraint(a, pltpu.HBM)
            for a in (master, gradient, first_moment, second_moment)
        ),
    )
    new_master, new_first, new_second, whole = (
        pltpu.with_memory_space_constraint(a, pltpu.VMEM) for a in held
    )
    codes, block_scales, new_master, new_first, new_second = pl.pallas_call(
        write_kernel,
        out_shape=(
            jax.ShapeDtypeStruct((kept, cols), BF16),
            jax.ShapeDtypeStruct((kept, scales), BF16),
        )
        + tuple(jax.ShapeDtypeStruct((rows, width), F32) for _ in range(3)),
        in_specs=[vmem] * 4,
        out_specs=tuple(any_spec for _ in range(5)),
        scratch_shapes=[pltpu.SemaphoreType.DMA((12,))],
        compiler_params=pltpu.CompilerParams(vmem_limit_bytes=16 * 2**20),
        name="write_results",
    )(whole, new_master, new_first, new_second)
    return (new_master, new_first, new_second, codes, block_scales)


def solution(mesh):
    return jax.shard_map(
        per_device,
        mesh=mesh,
        in_specs=(P("shard", "pair"),) * 4 + (P(), P()),
        out_specs=(P("shard", "pair"),) * 3 + (P("pair", None),) * 2,
        check_vma=False,
    )
```

time: 181 us -> 83.1 us (0.46)
  waiting for transfers between devices: 93.8 us -> 0 us
  Pallas kernels: 0 us -> 79.6 us
  blocking collectives: 51.4 us -> 0 us
  between operations: 16.2 us -> 1.93 us
  local copies, waits for them, and re-layouts: 13.7 us -> 0 us
  other arithmetic: 5.51 us -> 0 us
    all_gather x1 -> x0, waiting for transfers between devices: 93.8 us -> none  [side_by_side(): whole = lax.all_gather(both, axis, axis=dim, tiled=True)]
    pallas_call x0 -> x2, Pallas kernels: none -> 79.6 us  [the longest x1 74.4 us: per_device(): pl.pallas_call(gather_kernel, out_shape=tuple((pltpu.VMEM((rows, width),...]
    psum x4 -> x0, blocking collectives: 33.1 us -> none  [by_axis(): return functools.reduce(lax.psum, axes, x)]
    all_to_all x2 -> x0, blocking collectives: 18.3 us -> none  [the longest x1 13.8 us: per_device(): lax.all_to_all(half_codes, 'pair', split_axis=0, concat_axis=1, tiled=True)]
    split x3 -> x0, local copies, waits for them, and re-layouts: 5.76 us -> none  [side_by_side(): jnp.split(whole, [sum(widths[:k]) for k in range(1, len(widths))], axis=a...]
    all_to_all x2 -> x0, local copies, waits for them, and re-layouts: 5.31 us -> none  [the longest x1 5.05 us: per_device(): lax.all_to_all(half_codes, 'pair', split_axis=0, concat_axis=1, tiled=True)]
    abs x1 -> x0, other arithmetic: 2.55 us -> none  [quantize(): largest = jnp.max(jnp.abs(blocked), axis=2)]
  transfers between devices with their start and end apart: 1 -> 0, of which waited for: 1 -> 0; matrix products, arithmetic and copies ran while one was open for 0% -> 0% of each run, Pallas kernels for 0% -> 0%
where the time goes in v1:
time: 83.1 us; the launch traced here: 81.5 us
  Pallas kernels  79.6 us (96%)
  between operations  1.93 us (2%)
    pallas_call x1, Pallas kernels, per_device(): pl.pallas_call(gather_kernel, out_shape=tuple((pltpu.VMEM((rows, width),...  74.4 us
    pallas_call x1, Pallas kernels, per_device(): pl.pallas_call(write_kernel, out_shape=(jax.ShapeDtypeStruct((kept, cols)...  5.13 us

profile of v1, /device:TPU:1, one launch (start us, length us, event | category | flops | bytes accessed | tf_op | source)
XLA Modules:
  0.0 81.5 jit_solution(5358679523381890633)
XLA Ops:
  1.9 74.4 %update_and_gather.1 = (f32[48,2048]{1,0:T(8,128)S(1)}, f32[48,2048]{1,0:T(8,128)S(1)}, f32[48,2048]{1,0:T(8,128)S(1)}, bf16[1536,4224]{1,0:T(8,128)(2,1)S(1)}) custom-call(f32[1]{0:T(128)S(6)} %copy.11.max_norm, s32[1]{0:T(128)S(6)} %copy.12.step_count, f32[48,2048]{1,0:T(8,128)} %master.1, f32[48,2048]{1,0:T(8,128)} %gradient.1, f32[48,2048]{1,0:T(8,128)} %first.1, ...), custom_call_target="tpu_custom_call" | custom-call | tf_op jit(solution)/shard_map/update_and_gather/pallas_call | solution.py:399
  76.4 5.1 %write_results.1 = (bf16[1536,4096]{1,0:T(8,128)(2,1)}, bf16[1536,128]{1,0:T(8,128)(2,1)}, f32[48,2048]{1,0:T(8,128)}, f32[48,2048]{1,0:T(8,128)}, f32[48,2048]{1,0:T(8,128)}) custom-call(bf16[1536,4224]{1,0:T(8,128)(2,1)S(1)} %get-tuple-element.14.whole, f32[48,2048]{1,0:T(8,128)S(1)} %get-tuple-element.15.new_master, ...), custom_call_target="tpu_custom_call" | custom-call | tf_op jit(solution)/shard_map/write_results/pallas_call | solution.py:429

commit v2 on v1

--- a/solution.py
+++ b/solution.py
@@ -107,6 +107,8 @@
     whole,
     own,
     other,
+    fresh,
+    largest,
     sums,
     sum_rx,
     load_sem,
@@ -164,8 +166,8 @@
             pltpu.make_async_remote_copy(
                 src_ref=sums.at[step],
                 dst_ref=sum_rx.at[base + k],
-                send_sem=sum_send.at[base + k],
-                recv_sem=sum_recv.at[base + k],
+                send_sem=sum_send.at[step],
+                recv_sem=sum_recv.at[step],
                 device_id=peer,
                 device_id_type=MESH,
             )
@@ -173,21 +175,26 @@
         ]
         for copy in copies:
             copy.start()
-        return copies
-
-    swaps = [
-        pltpu.make_async_remote_copy(
-            src_ref=own.at[k],
-            dst_ref=other.at[k],
-            send_sem=swap_sem.at[k],
-            recv_sem=swap_sem.at[4 + k],
-            device_id=partner,
+        slots = sum_rx.at[pl.ds(base, len(to))]
+        return pltpu.make_async_remote_copy(
+            src_ref=slots,
+            dst_ref=slots,
+            send_sem=sum_send.at[step],
+            recv_sem=sum_recv.at[step],
+            device_id=to[0],
             device_id_type=MESH,
         )
-        for k in range(4)
-    ]
-
-    copies = []
+
+    swap = pltpu.make_async_remote_copy(
+        src_ref=own,
+        dst_ref=other,
+        send_sem=swap_sem.at[0],
+        recv_sem=swap_sem.at[1],
+        device_id=partner,
+        device_id_type=MESH,
+    )
+
+    exchanges = []
     base = 0
     for step, to in enumerate((x_peers, y_peers, z_peers)):
         started = exchange(step, base, to)
@@ -195,16 +202,14 @@
 
             @pl.when(jnp.logical_not(source))
             def _():
-                for swap in swaps:
-                    swap.start()
-
-        for k, copy in enumerate(started):
-            copy.wait_recv()
+                swap.start()
+
+        started.wait_recv()
         acc = sums[step]
         for k in range(len(to)):
             acc = acc + sum_rx[base + k]
         base += len(to)
-        copies += started
+        exchanges.append(started)
         if step < 2:
             sums[step + 1] = acc
 
@@ -219,8 +224,7 @@
     inv_second = jnp.broadcast_to(inv_second, (PART, LANES))
 
     lane = lax.broadcasted_iota(jnp.int32, (PART, LANES), 1)
-    bits = [(s, lax.bitwise_and(lane, s) != 0) for s in (1, 2, 4, 8, 16)]
-    in_block = lax.bitwise_and(lane, BLOCK - 1)
+    block_start = lane - lax.bitwise_and(lane, BLOCK - 1)
     to_lane = lax.broadcasted_iota(jnp.int32, (LANES, LANES), 1)
     from_lane = lax.broadcasted_iota(jnp.int32, (LANES, LANES), 0)
     spread = jnp.where(
@@ -243,16 +247,49 @@
         new_first[pl.ds(i, PART), pl.ds(j, LANES)] = m
         new_second[pl.ds(i, PART), pl.ds(j, LANES)] = v
 
-    def quantize(row, half, tile, w, scales):
-        largest = jnp.abs(w)
-        for s, bit in bits:
-            lower = pltpu.roll(largest, s, 1)
-            upper = pltpu.roll(largest, LANES - s, 1)
-            largest = jnp.maximum(largest, jnp.where(bit, lower, upper))
-        scale = jnp.maximum(largest, scale_floor).astype(BF16).astype(F32)
-        column = pl.multiple_of(half * width + tile * LANES, LANES)
-        whole[pl.ds(row, PART), pl.ds(column, LANES)] = (w / scale).astype(BF16)
-        return jnp.where(in_block == half * tiles + tile, scale, scales)
+    def merge(a, b, bit):
+        here = lax.bitwise_and(lane, bit) != 0
+        crossed = jnp.where(here, a, b)
+        crossed = jnp.where(here, pltpu.roll(crossed, bit, 1), pltpu.roll(crossed, LANES - bit, 1))
+        return jnp.maximum(jnp.where(here, b, a), crossed)
+
+    def merge_all(values, bit):
+        while len(values) > 1:
+            values = [merge(a, b, bit) for a, b in zip(values[::2], values[1::2])]
+            bit *= 2
+        return values[0]
+
+    def update_chunk(i, row):
+        def update(t, carry):
+            for half, held in enumerate((own, other)):
+                at_half = core if half == 0 else 1 - core
+                sizes = []
+                for k in range(step_tiles):
+                    j = pl.multiple_of((t * step_tiles + k) * LANES, LANES)
+                    w, m, v = adam(held, i, j)
+                    if half == 0:
+                        store(i, j, w, m, v)
+                    fresh[:, pl.ds(pl.multiple_of(at_half * width + j, LANES), LANES)] = w
+                    sizes.append(jnp.abs(w))
+                largest[half, t] = merge_all(sizes, 1)
+            return carry
+
+        lax.fori_loop(0, tiles // step_tiles, update, 0)
+        mine, others = (merge_all([largest[h, t] for t in range(tiles // step_tiles)], step_tiles) for h in (0, 1))
+        top = merge(jnp.where(core == 0, mine, others), jnp.where(core == 0, others, mine), tiles)
+        scales = jnp.maximum(top, scale_floor).astype(BF16)
+        whole[pl.ds(row, PART), cols:] = jnp.dot(scales, spread, preferred_element_type=F32).astype(BF16)
+        inverse = 1.0 / scales.astype(F32)
+
+        def code(t, carry):
+            for k in range(2 * step_tiles):
+                tile = t * 2 * step_tiles + k
+                j = pl.ds(pl.multiple_of(tile * LANES, LANES), LANES)
+                by = jnp.take_along_axis(inverse, block_start + tile, axis=1, mode="promise_in_bounds")
+                whole[pl.ds(row, PART), j] = (fresh[:, j] * by).astype(BF16)
+            return carry
+
+        lax.fori_loop(0, tiles // step_tiles, code, 0)
 
     line = [[(lax.rem(y + 4 - oy, 4) * 4 + lax.rem(x + 4 - ox, 4)) * rows for oy in range(4)] for ox in range(4)]
     plane_row = [jnp.where(flip, 16 * rows, 0), jnp.where(flip, 0, 16 * rows)]
@@ -270,7 +307,10 @@
         p, plane, ox, oy = chunk
         return whole.at[pl.ds(pl.multiple_of(line[ox][oy] + plane_row[plane] + p * PART, PART), PART), pieces[half]]
 
-    def piece(chunk, half, role_now, d, s, number):
+    def lane_of(d, s, half):
+        return (d * 2 + (s < 0)) * 3 + half
+
+    def piece(chunk, half, role_now, d, s):
         p, plane, ox, oy = chunk
         if d == 0:
             ox = (ox + s) % 4
@@ -282,7 +322,7 @@
         return pltpu.make_async_remote_copy(
             src_ref=ref,
             dst_ref=ref,
-            send_sem=send_sem.at[number],
+            send_sem=send_sem.at[lane_of(d, s, half)],
             recv_sem=recv_sem.at[slot((p, plane, ox, oy), half)],
             device_id=(core, near[(d, s)]),
             device_id_type=MESH,
@@ -308,41 +348,33 @@
             if 0 in seen or len(seen) == 2:
                 p, plane, ox, oy = chunk
                 for d, s, h in hops(p, plane, (ox, oy, (role_now - plane) % 4)):
-                    copy = piece(chunk, h, role_now, d, s, len(sent))
-                    copy.start()
-                    sent.append(copy)
-        for copy in sent:
-            copy.wait_send()
+                    piece(chunk, h, role_now, d, s).start()
+                    sent.append((d, s, h))
+        for d, s, h in sorted(set(sent)):
+            total = whole.at[pl.ds(0, PART * sent.count((d, s, h))), pieces[h]]
+            pltpu.make_async_remote_copy(
+                src_ref=total,
+                dst_ref=total,
+                send_sem=send_sem.at[lane_of(d, s, h)],
+                recv_sem=recv_sem.at[0],
+                device_id=(core, near[(d, s)]),
+                device_id_type=MESH,
+            ).wait_send()
 
     schedule = arrivals()
 
     @pl.when(source)
     def _():
-        for swap in swaps:
-            swap.wait_recv()
+        swap.wait_recv()
         sent = []
         for p in range(parts):
             i = p * PART
             row = pl.multiple_of(line[0][0] + plane_row[0] + i, PART)
 
-            def body(t, scales, i=i, row=row):
-                for k in range(step_tiles):
-                    tile = t * step_tiles + k
-                    j = pl.multiple_of(tile * LANES, LANES)
-                    w, m, v = adam(own, i, j)
-                    store(i, j, w, m, v)
-                    scales = quantize(row, core, tile, w, scales)
-                    w, m, v = adam(other, i, j)
-                    scales = quantize(row, 1 - core, tile, w, scales)
-                return scales
-
-            scales = lax.fori_loop(0, tiles // step_tiles, body, jnp.zeros((PART, LANES), F32))
-            moved = jnp.dot(scales.astype(BF16), spread, preferred_element_type=F32)
-            whole[pl.ds(row, PART), cols:] = moved.astype(BF16)
+            update_chunk(i, row)
             for d, s, h in hops(p, 0, (0, 0, 0)):
-                copy = piece((p, 0, 0, 0), h, 0, d, s, len(sent))
-                copy.start()
-                sent.append(copy)
+                piece((p, 0, 0, 0), h, 0, d, s).start()
+                sent.append((d, s, h))
         follow(0, schedule[0], sent)
 
     @pl.when(jnp.logical_not(source))
@@ -358,11 +390,10 @@
 
             lax.fori_loop(0, tiles // step_tiles, body, 0)
         follow(3, schedule[3], [])
-        for swap in swaps:
-            swap.wait_send()
-
-    for copy in copies:
-        copy.wait_send()
+        swap.wait_send()
+
+    for started in exchanges:
+        started.wait_send()
 
 
 def write_kernel(whole, new_master, new_first, new_second, codes_out, scales_out, master_out, first_out, second_out, sem):
@@ -395,7 +426,6 @@
     smem = pl.BlockSpec(memory_space=pltpu.SMEM)
     any_spec = pl.BlockSpec(memory_space=pl.ANY)
     vmem = pl.BlockSpec(memory_space=pltpu.VMEM)
-    sends = 160
     held = pl.pallas_call(
         gather_kernel,
         out_shape=tuple(pltpu.VMEM((rows, width), F32) for _ in range(3)) + (pltpu.VMEM((kept, full), BF16),),
@@ -404,13 +434,15 @@
         scratch_shapes=[
             pltpu.VMEM((4, rows, width), F32),
             pltpu.VMEM((4, rows, width), F32),
+            pltpu.VMEM((PART, cols), F32),
+            pltpu.VMEM((2, 4, PART, LANES), F32),
             pltpu.VMEM((3, 8, LANES), F32),
             pltpu.VMEM((13, 8, LANES), F32),
             pltpu.SemaphoreType.DMA((4,)),
-            pltpu.SemaphoreType.DMA((8,)),
-            pltpu.SemaphoreType.DMA((13,)),
-            pltpu.SemaphoreType.DMA((13,)),
-            pltpu.SemaphoreType.DMA((sends,)),
+            pltpu.SemaphoreType.DMA((2,)),
+            pltpu.SemaphoreType.DMA((3,)),
+            pltpu.SemaphoreType.DMA((3,)),
+            pltpu.SemaphoreType.DMA((18,)),
             pltpu.SemaphoreType.DMA((SLOTS,)),
         ],
         compiler_params=pltpu.CompilerParams(collective_id=0, has_side_effects=True, vmem_limit_bytes=16 * 2**20),

time: 83.1 us -> 80.7 us (0.971)
  Pallas kernels: 79.6 us -> 77.4 us
    pallas_call x1, Pallas kernels: 74.4 us -> 72.3 us  [per_device(): pl.pallas_call(gather_kernel, out_shape=tuple((pltpu.VMEM((rows, width),...]
where the time goes in v2:
time: 80.7 us; the launch traced here: 79.4 us
  Pallas kernels  77.4 us (96%)
  between operations  1.93 us (2%)
    pallas_call x1, Pallas kernels, per_device(): pl.pallas_call(gather_kernel, out_shape=tuple((pltpu.VMEM((rows, width),...  72.3 us
    pallas_call x1, Pallas kernels, per_device(): pl.pallas_call(write_kernel, out_shape=(jax.ShapeDtypeStruct((kept, cols)...  5.13 us

profile of v2, /device:TPU:1, one launch (start us, length us, event | category | flops | bytes accessed | tf_op | source)
XLA Modules:
  0.0 79.4 jit_solution(8261445030872363613)
XLA Ops:
  1.9 72.3 %update_and_gather.1 = (f32[48,2048]{1,0:T(8,128)S(1)}, f32[48,2048]{1,0:T(8,128)S(1)}, f32[48,2048]{1,0:T(8,128)S(1)}, bf16[1536,4224]{1,0:T(8,128)(2,1)S(1)}) custom-call(f32[1]{0:T(128)S(6)} %copy.11.max_norm, s32[1]{0:T(128)S(6)} %copy.12.step_count, f32[48,2048]{1,0:T(8,128)} %master.1, f32[48,2048]{1,0:T(8,128)} %gradient.1, f32[48,2048]{1,0:T(8,128)} %first.1, ...), custom_call_target="tpu_custom_call" | custom-call | tf_op jit(solution)/shard_map/update_and_gather/pallas_call | solution.py:429
  74.2 5.1 %write_results.1 = (bf16[1536,4096]{1,0:T(8,128)(2,1)}, bf16[1536,128]{1,0:T(8,128)(2,1)}, f32[48,2048]{1,0:T(8,128)}, f32[48,2048]{1,0:T(8,128)}, f32[48,2048]{1,0:T(8,128)}) custom-call(bf16[1536,4224]{1,0:T(8,128)(2,1)S(1)} %get-tuple-element.14.whole, f32[48,2048]{1,0:T(8,128)S(1)} %get-tuple-element.15.new_master, ...), custom_call_target="tpu_custom_call" | custom-call | tf_op jit(solution)/shard_map/write_results/pallas_call | solution.py:461

commit v3 on v2

--- a/solution.py
+++ b/solution.py
@@ -86,12 +86,21 @@
                     queues[(r, d, s)].append((chunk, h))
 
 
-def slot(chunk, half):
+def is_leaf(role, chunk):
     p, plane, ox, oy = chunk
-    return (((p * 2 + plane) * 4 + ox) * 4 + oy) * 2 + (half == 2)
-
-
-SLOTS = 3 * 2 * 4 * 4 * 2
+    return not hops(p, plane, (ox, oy, (role - plane) % 4))
+
+
+SCHEDULE = arrivals()
+SLOTS = {
+    role: {piece: n for n, piece in enumerate(p for p in SCHEDULE[role] if not is_leaf(role, p[0]))}
+    for role in (0, 3)
+}
+LEAVES = max(len(s) for s in SLOTS.values())
+
+
+def slot(role, chunk, half):
+    return LEAVES + (half == 2) if is_leaf(role, chunk) else SLOTS[role][(chunk, half)]
 
 
 def gather_kernel(
@@ -312,37 +321,42 @@
 
     def piece(chunk, half, role_now, d, s):
         p, plane, ox, oy = chunk
+        role = role_now
         if d == 0:
             ox = (ox + s) % 4
         elif d == 1:
             oy = (oy + s) % 4
         elif (role_now == 0) == (s == 1):
             plane = 1 - plane
+        else:
+            role = 3 - role_now
         ref = place(chunk, half)
         return pltpu.make_async_remote_copy(
             src_ref=ref,
             dst_ref=ref,
             send_sem=send_sem.at[lane_of(d, s, half)],
-            recv_sem=recv_sem.at[slot((p, plane, ox, oy), half)],
+            recv_sem=recv_sem.at[slot(role, (p, plane, ox, oy), half)],
             device_id=(core, near[(d, s)]),
             device_id_type=MESH,
         )
 
-    def landed(chunk, half):
-        ref = place(chunk, half)
+    def landed(number, ref):
         pltpu.make_async_remote_copy(
             src_ref=ref,
             dst_ref=ref,
             send_sem=send_sem.at[0],
-            recv_sem=recv_sem.at[slot(chunk, half)],
+            recv_sem=recv_sem.at[number],
             device_id=(core, near[(0, 1)]),
             device_id_type=MESH,
         ).wait_recv()
 
     def follow(role_now, order, sent):
         got = {}
+        leaves = [h for chunk, h in order if is_leaf(role_now, chunk)]
         for chunk, half in order:
-            landed(chunk, half)
+            if is_leaf(role_now, chunk):
+                continue
+            landed(slot(role_now, chunk, half), place(chunk, half))
             seen = got.setdefault(chunk, set())
             seen.add(half)
             if 0 in seen or len(seen) == 2:
@@ -350,6 +364,8 @@
                 for d, s, h in hops(p, plane, (ox, oy, (role_now - plane) % 4)):
                     piece(chunk, h, role_now, d, s).start()
                     sent.append((d, s, h))
+        for h in sorted(set(leaves)):
+            landed(LEAVES + (h == 2), whole.at[pl.ds(0, PART * leaves.count(h)), pieces[h]])
         for d, s, h in sorted(set(sent)):
             total = whole.at[pl.ds(0, PART * sent.count((d, s, h))), pieces[h]]
             pltpu.make_async_remote_copy(
@@ -361,8 +377,6 @@
                 device_id_type=MESH,
             ).wait_send()
 
-    schedule = arrivals()
-
     @pl.when(source)
     def _():
         swap.wait_recv()
@@ -375,7 +389,7 @@
             for d, s, h in hops(p, 0, (0, 0, 0)):
                 piece((p, 0, 0, 0), h, 0, d, s).start()
                 sent.append((d, s, h))
-        follow(0, schedule[0], sent)
+        follow(0, SCHEDULE[0], sent)
 
     @pl.when(jnp.logical_not(source))
     def _():
@@ -389,7 +403,7 @@
                 return carry
 
             lax.fori_loop(0, tiles // step_tiles, body, 0)
-        follow(3, schedule[3], [])
+        follow(3, SCHEDULE[3], [])
         swap.wait_send()
 
     for started in exchanges:
@@ -443,7 +457,7 @@
             pltpu.SemaphoreType.DMA((3,)),
             pltpu.SemaphoreType.DMA((3,)),
             pltpu.SemaphoreType.DMA((18,)),
-            pltpu.SemaphoreType.DMA((SLOTS,)),
+            pltpu.SemaphoreType.DMA((LEAVES + 2,)),
         ],
         compiler_params=pltpu.CompilerParams(collective_id=0, has_side_effects=True, vmem_limit_bytes=16 * 2**20),
         name="update_and_gather",

time: 80.7 us -> 78.6 us (0.974); the launches traced: 79.4 us -> 78.4 us
  Pallas kernels: 77.4 us -> 76.5 us
    pallas_call x1, Pallas kernels: 72.3 us -> 71.4 us  [per_device(): pl.pallas_call(gather_kernel, out_shape=tuple((pltpu.VMEM((rows, width),...]
where the time goes in v3:
time: 78.6 us; the launch traced here: 78.4 us
  Pallas kernels  76.5 us (97%)
  between operations  1.93 us (2%)
    pallas_call x1, Pallas kernels, per_device(): pl.pallas_call(gather_kernel, out_shape=tuple((pltpu.VMEM((rows, width),...  71.4 us
    pallas_call x1, Pallas kernels, per_device(): pl.pallas_call(write_kernel, out_shape=(jax.ShapeDtypeStruct((kept, cols)...  5.13 us

profile of v3, /device:TPU:1, one launch (start us, length us, event | category | flops | bytes accessed | tf_op | source)
XLA Modules:
  0.0 78.4 jit_solution(2754624117583981921)
XLA Ops:
  1.9 71.4 %update_and_gather.1 = (f32[48,2048]{1,0:T(8,128)S(1)}, f32[48,2048]{1,0:T(8,128)S(1)}, f32[48,2048]{1,0:T(8,128)S(1)}, bf16[1536,4224]{1,0:T(8,128)(2,1)S(1)}) custom-call(f32[1]{0:T(128)S(6)} %copy.11.max_norm, s32[1]{0:T(128)S(6)} %copy.12.step_count, f32[48,2048]{1,0:T(8,128)} %master.1, f32[48,2048]{1,0:T(8,128)} %gradient.1, f32[48,2048]{1,0:T(8,128)} %first.1, ...), custom_call_target="tpu_custom_call" | custom-call | tf_op jit(solution)/shard_map/update_and_gather/pallas_call | solution.py:443
  73.3 5.1 %write_results.1 = (bf16[1536,4096]{1,0:T(8,128)(2,1)}, bf16[1536,128]{1,0:T(8,128)(2,1)}, f32[48,2048]{1,0:T(8,128)}, f32[48,2048]{1,0:T(8,128)}, f32[48,2048]{1,0:T(8,128)}) custom-call(bf16[1536,4224]{1,0:T(8,128)(2,1)S(1)} %get-tuple-element.14.whole, f32[48,2048]{1,0:T(8,128)S(1)} %get-tuple-element.15.new_master, ...), custom_call_target="tpu_custom_call" | custom-call | tf_op jit(solution)/shard_map/write_results/pallas_call | solution.py:475

commit v4 on v3

--- a/solution.py
+++ b/solution.py
@@ -145,11 +145,10 @@
         return lax.rem(zz, 4) * 16 + lax.rem(yy, 4) * 4 + lax.rem(xx, 4)
 
     partner = (1 - core, me)
-    x_peers = [(k, at(x + dx, y, z)) for dx in (1, 2, 3) for k in (core, 1 - core)] + [partner]
-    y_peers = [(core, at(x, y + d, z)) for d in (1, 2, 3)]
-    z_peers = [(core, at(x, y, z + d)) for d in (1, 2, 3)]
+    plane_peers = [(core, at(x + dx, y + dy, z)) for dx in (2, 1, 3, 0) for dy in (2, 1, 3, 0) if dx or dy]
+    line_peers = [(k, at(x, y, z + d)) for d in (2, 1, 3) for k in (1 - core, core)] + [partner]
     barrier = pltpu.get_barrier_semaphore()
-    peers = x_peers + y_peers + z_peers
+    peers = plane_peers + line_peers
     for peer in peers:
         pl.semaphore_signal(barrier, inc=1, device_id=peer, device_id_type=MESH)
 
@@ -165,7 +164,7 @@
         for j in range(0, width, LANES):
             g = own[0, i : i + 8, j : j + LANES]
             acc = acc + g * g
-    sums[0] = acc
+    sums[0] = jnp.sum(acc, axis=0, keepdims=True)
     for load in loads[1:]:
         load.wait()
     pl.semaphore_wait(barrier, len(peers))
@@ -205,7 +204,7 @@
 
     exchanges = []
     base = 0
-    for step, to in enumerate((x_peers, y_peers, z_peers)):
+    for step, to in enumerate((plane_peers, line_peers)):
         started = exchange(step, base, to)
         if step == 0:
 
@@ -219,7 +218,7 @@
             acc = acc + sum_rx[base + k]
         base += len(to)
         exchanges.append(started)
-        if step < 2:
+        if step < 1:
             sums[step + 1] = acc
 
     squares = jnp.sum(acc, axis=(0, 1), keepdims=True)
@@ -450,12 +449,12 @@
             pltpu.VMEM((4, rows, width), F32),
             pltpu.VMEM((PART, cols), F32),
             pltpu.VMEM((2, 4, PART, LANES), F32),
-            pltpu.VMEM((3, 8, LANES), F32),
-            pltpu.VMEM((13, 8, LANES), F32),
+            pltpu.VMEM((2, 1, LANES), F32),
+            pltpu.VMEM((22, 1, LANES), F32),
             pltpu.SemaphoreType.DMA((4,)),
             pltpu.SemaphoreType.DMA((2,)),
-            pltpu.SemaphoreType.DMA((3,)),
-            pltpu.SemaphoreType.DMA((3,)),
+            pltpu.SemaphoreType.DMA((2,)),
+            pltpu.SemaphoreType.DMA((2,)),
             pltpu.SemaphoreType.DMA((18,)),
             pltpu.SemaphoreType.DMA((LEAVES + 2,)),
         ],

time: 78.6 us -> 77.2 us (0.982)
  Pallas kernels: 76.5 us -> 75.1 us
    pallas_call x1, Pallas kernels: 71.4 us -> 69.9 us  [per_device(): pl.pallas_call(gather_kernel, out_shape=tuple((pltpu.VMEM((rows, width),...]
where the time goes in v4:
time: 77.2 us; the launch traced here: 77 us
  Pallas kernels  75.1 us (97%)
  between operations  1.93 us (2%)
    pallas_call x1, Pallas kernels, per_device(): pl.pallas_call(gather_kernel, out_shape=tuple((pltpu.VMEM((rows, width),...  69.9 us
    pallas_call x1, Pallas kernels, per_device(): pl.pallas_call(write_kernel, out_shape=(jax.ShapeDtypeStruct((kept, cols)...  5.13 us

profile of v4, /device:TPU:1, one launch (start us, length us, event | category | flops | bytes accessed | tf_op | source)
XLA Modules:
  0.0 77.0 jit_solution(12590534572587254684)
XLA Ops:
  1.9 69.9 %update_and_gather.1 = (f32[48,2048]{1,0:T(8,128)S(1)}, f32[48,2048]{1,0:T(8,128)S(1)}, f32[48,2048]{1,0:T(8,128)S(1)}, bf16[1536,4224]{1,0:T(8,128)(2,1)S(1)}) custom-call(f32[1]{0:T(128)S(6)} %copy.11.max_norm, s32[1]{0:T(128)S(6)} %copy.12.step_count, f32[48,2048]{1,0:T(8,128)} %master.1, f32[48,2048]{1,0:T(8,128)} %gradient.1, f32[48,2048]{1,0:T(8,128)} %first.1, ...), custom_call_target="tpu_custom_call" | custom-call | tf_op jit(solution)/shard_map/update_and_gather/pallas_call | solution.py:442
  71.9 5.1 %write_results.1 = (bf16[1536,4096]{1,0:T(8,128)(2,1)}, bf16[1536,128]{1,0:T(8,128)(2,1)}, f32[48,2048]{1,0:T(8,128)}, f32[48,2048]{1,0:T(8,128)}, f32[48,2048]{1,0:T(8,128)}) custom-call(bf16[1536,4224]{1,0:T(8,128)(2,1)S(1)} %get-tuple-element.14.whole, f32[48,2048]{1,0:T(8,128)S(1)} %get-tuple-element.15.new_master, ...), custom_call_target="tpu_custom_call" | custom-call | tf_op jit(solution)/shard_map/write_results/pallas_call | solution.py:474

commit v5 on v4

--- a/solution.py
+++ b/solution.py
@@ -42,7 +42,7 @@
     return out
 
 
-def arrivals(unit=1.45, latency=1.7, ready=(0.6, 1.2, 1.8)):
+def arrivals(unit=1.5, latency=2.8, ready=(1.65, 3.3, 4.95)):
     queues = {(r, d, s): [] for r in range(4) for d in range(3) for s in (1, -1)}
     heads, events, count, now = {}, [], itertools.count(), 0.0
     got = {r: {} for r in range(4)}
@@ -233,11 +233,8 @@
 
     lane = lax.broadcasted_iota(jnp.int32, (PART, LANES), 1)
     block_start = lane - lax.bitwise_and(lane, BLOCK - 1)
-    to_lane = lax.broadcasted_iota(jnp.int32, (LANES, LANES), 1)
-    from_lane = lax.broadcasted_iota(jnp.int32, (LANES, LANES), 0)
-    spread = jnp.where(
-        lax.div(from_lane, BLOCK) + (LANES // BLOCK) * lax.rem(from_lane, BLOCK) == to_lane, 1.0, 0.0
-    ).astype(BF16)
+    per_tile = LANES // BLOCK
+    gathered = BLOCK * lax.rem(lane, per_tile) + lax.div(lane, per_tile)
 
     def adam(held, i, j):
         g, m, v, w = (held[k, pl.ds(i, PART), pl.ds(j, LANES)] for k in range(4))
@@ -285,9 +282,10 @@
         lax.fori_loop(0, tiles // step_tiles, update, 0)
         mine, others = (merge_all([largest[h, t] for t in range(tiles // step_tiles)], step_tiles) for h in (0, 1))
         top = merge(jnp.where(core == 0, mine, others), jnp.where(core == 0, others, mine), tiles)
-        scales = jnp.maximum(top, scale_floor).astype(BF16)
-        whole[pl.ds(row, PART), cols:] = jnp.dot(scales, spread, preferred_element_type=F32).astype(BF16)
-        inverse = 1.0 / scales.astype(F32)
+        scales = jnp.maximum(top, scale_floor).astype(BF16).astype(F32)
+        inverse = 1.0 / scales
+        in_order = jnp.take_along_axis(scales, gathered, axis=1, mode="promise_in_bounds")
+        whole[pl.ds(row, PART), cols:] = in_order.astype(BF16)
 
         def code(t, carry):
             for k in range(2 * step_tiles):

time: 77.2 us -> 76.9 us (level)
  no operation moved by 1% of the time
where the time goes in v5:
time: 76.9 us; the launch traced here: 76.8 us
  Pallas kernels  74.8 us (97%)
  between operations  1.93 us (3%)
    pallas_call x1, Pallas kernels, per_device(): pl.pallas_call(gather_kernel, out_shape=tuple((pltpu.VMEM((rows, width),...  69.7 us
    pallas_call x1, Pallas kernels, per_device(): pl.pallas_call(write_kernel, out_shape=(jax.ShapeDtypeStruct((kept, cols)...  5.13 us

profile of v5, /device:TPU:1, one launch (start us, length us, event | category | flops | bytes accessed | tf_op | source)
XLA Modules:
  0.0 76.8 jit_solution(14635827975060343570)
XLA Ops:
  1.9 69.7 %update_and_gather.1 = (f32[48,2048]{1,0:T(8,128)S(1)}, f32[48,2048]{1,0:T(8,128)S(1)}, f32[48,2048]{1,0:T(8,128)S(1)}, bf16[1536,4224]{1,0:T(8,128)(2,1)S(1)}) custom-call(f32[1]{0:T(128)S(6)} %copy.11.max_norm, s32[1]{0:T(128)S(6)} %copy.12.step_count, f32[48,2048]{1,0:T(8,128)} %master.1, f32[48,2048]{1,0:T(8,128)} %gradient.1, f32[48,2048]{1,0:T(8,128)} %first.1, ...), custom_call_target="tpu_custom_call" | custom-call | tf_op jit(solution)/shard_map/update_and_gather/pallas_call | solution.py:440
  71.6 5.1 %write_results.1 = (bf16[1536,4096]{1,0:T(8,128)(2,1)}, bf16[1536,128]{1,0:T(8,128)(2,1)}, f32[48,2048]{1,0:T(8,128)}, f32[48,2048]{1,0:T(8,128)}, f32[48,2048]{1,0:T(8,128)}) custom-call(bf16[1536,4224]{1,0:T(8,128)(2,1)S(1)} %get-tuple-element.14.whole, f32[48,2048]{1,0:T(8,128)S(1)} %get-tuple-element.15.new_master, ...), custom_call_target="tpu_custom_call" | custom-call | tf_op jit(solution)/shard_map/write_results/pallas_call | solution.py:472
